TPU v7x, 32 devices: a whole 2x2x4 slice. The times are simulated.
32 devices in a mesh: grp: 8 (over y, x, core), shard: 4 (over z).
Axes of the slice: x: 2, y: 2, z: 4, core: 2. Of those that a mesh axis runs over, the one named last changes fastest.
Arguments:
- gradients: bfloat16 [8, 1024, 5120], P('grp', None, 'shard'), may hold values from -150 to 150
- left_factor: bfloat16 [8, 1024, 1024], P('grp'), may hold values from -1 to 2, as said below
- right_factor: bfloat16 [8, 5120, 5120], P('grp', 'shard'), may hold values from -1 to 2, as said below
Outputs:
- update: bfloat16 [8, 1024, 5120], P('grp', None, 'shard')
Inputs may be any that keep to these rules, and one draw needn't show every extreme that they name: `left_factor`: each factor is upper triangular with a positive diagonal. `right_factor`: each factor is upper triangular with a positive diagonal.
All inputs are finite; a program needn't handle non-finite values.
Results may differ from a plain program's by a relative error of at most 0.0061.
Values may be sent and summed in bfloat16 or wider, within the bound.
A program may use at most 128 MiB of HBM per device.

v0:
```python
import jax
import jax.numpy as jnp
from jax import lax
from jax.sharding import PartitionSpec as P


def body(gradients, left_factor, right_factor):
    squares = jnp.float32(0.0)
    gradient = gradients[0]
    left_q = left_factor[0]
    right_rows = right_factor[0]
    block = right_rows
    first = lax.dot_general(
        lax.all_gather(gradient, "shard", axis=1, tiled=True),
        block,
        (((1,), (1,)), ((), ())),
        preferred_element_type=jnp.float32,
    ).astype(jnp.bfloat16)
    block = right_rows
    second_rows = lax.psum_scatter(
        lax.dot_general(block, first, (((0,), (1,)), ((), ())), preferred_element_type=jnp.float32),
        "shard",
        scatter_dimension=0,
        tiled=True,
    ).astype(jnp.bfloat16)
    second = second_rows.T
    third = jnp.dot(left_q, second, preferred_element_type=jnp.float32).astype(jnp.bfloat16)
    precond = lax.dot_general(
        left_q, third, (((0,), (0,)), ((), ())), preferred_element_type=jnp.float32
    )
    results = [precond]
    squares = jnp.sum(precond * precond)
    total = lax.psum(squares, ("grp", "shard"))
    count = (
        gradients.shape[0]
        * lax.axis_size("grp")
        * gradients.shape[1]
        * gradients.shape[2]
        * lax.axis_size("shard")
    )
    rms = jnp.sqrt(total / count + 1e-06)
    factor = jnp.minimum(jnp.float32(1.0), 1.1 / rms)
    stacked = jnp.stack(results, axis=0)
    return (stacked * factor).astype(jnp.bfloat16)


def solution(mesh):
    in_specs = (P("grp", None, "shard"), P("grp", None, None), P("grp", "shard", None))
    out_specs = P("grp", None, "shard")
    return jax.shard_map(body, mesh=mesh, in_specs=in_specs, out_specs=out_specs, check_vma=False)
```

profile of v0, /device:TPU:0, one launch (start us, length us, event | category | flops | bytes accessed | tf_op | source)
XLA Modules:
  0.0 647.6 jit_solution(3090217392802980609)
XLA Ops:
  6.5 0.0 copy-start
  6.5 0.0 all-gather.3.cloned.1.call-start
  6.5 0.7 all-gather.3.cloned.1.call-update
  7.3 0.0 reduce-scatter.2.cloned.1.call-start
  7.3 188.3 %all-gather.3.cloned.1.call-done = bf16[1,1024,5120]{2,1,0:T(8,128)(2,1)} async-done(((bf16[1,1024,1280]{2,1,0:T(8,128)(2,1)}), bf16[1,1024,5120]{2,1,0:T(8,128)(2,1)}) %all-gather.3.cloned.1.call-update) | async-done | bytes 10485776 | tf_op jit(solution)/shard_map/all_gather | solution.py:14
  195.6 17.5 %fusion.8 = bf16[1024,1280]{1,0:T(8,128)(2,1)S(1)} fusion(bf16[1,1280,5120]{2,1,0:T(8,128)(2,1)} %param.5, bf16[1,1024,5120]{2,1,0:T(8,128)(2,1)} %all-gather.3.cloned.1.call-done), kind=kOutput, calls=%fused_computation.8 | convolution fusion | flops 13423083520 | bytes 26214400 | tf_op jit(solution)/shard_map/dot_general | solution.py:13
  213.0 20.6 %fusion.4 = f32[5120,1024]{0,1:T(8,128)} fusion(bf16[1024,1280]{1,0:T(8,128)(2,1)S(1)} %fusion.8, bf16[1,1280,5120]{2,1,0:T(8,128)(2,1)} %param.5), kind=kOutput, calls=%fused_computation.4 | convolution fusion | flops 13421772800 | bytes 36700160 | tf_op jit(solution)/shard_map/dot_general | solution.py:21
  233.6 0.0 reduce-scatter.2.cloned.1.call-update
  233.7 345.7 %reduce-scatter.2.cloned.1.call-done = f32[1280,1024]{0,1:T(8,128)} async-done(((f32[5120,1024]{0,1:T(8,128)}), f32[1280,1024]{0,1:T(8,128)}) %reduce-scatter.2.cloned.1.call-update) | async-done | bytes 5242896 | tf_op jit(solution)/shard_map/reduce_scatter | solution.py:20
  579.4 0.0 copy-done
  579.4 9.9 %multiply_reduce_fusion = (f32[]{:T(128)}, f32[1280,1024]{1,0:T(8,128)}) fusion(bf16[1,1024,1024]{2,1,0:T(8,128)(2,1)S(1)} %copy-done, f32[1280,1024]{0,1:T(8,128)} %reduce-scatter.2.cloned.1.call-done), kind=kOutput, calls=%fused_computation.7 | convolution fusion | flops 5373952000 | bytes 12582916 | tf_op jit(solution)/shard_map/dot_general | solution.py:28
  589.3 41.7 %psum.7 = f32[]{:T(128)} all-reduce(f32[]{:T(128)} %get-tuple-element.5), channel_id=1, replica_groups=mesh['grp'=8,'shard'=4] {'grp','shard'}, use_global_device_ids=true, to_apply=%region_2.0 | all-reduce | flops 1 | bytes 8 | tf_op jit(solution)/shard_map/psum | solution.py:33
  631.7 4.7 fusion.13
  636.4 4.4 copy.4
Async XLA Ops:
  6.5 572.8 %copy-start = (bf16[1,1024,1024]{2,1,0:T(8,128)(2,1)S(1)}, bf16[1,1024,1024]{2,1,0:T(8,128)(2,1)}, u32[]{:S(2)}) copy-start(bf16[1,1024,1024]{2,1,0:T(8,128)(2,1)} %param.4) | copy-start | bytes 6291460
  6.5 189.0 %all-gather.3.cloned.1.call-start = ((), (), s32[]{:S(2)}) async-start(), calls=%async_computation.2 | async-start | bytes 13107200 | tf_op jit(solution)/shard_map/all_gather | solution.py:14
  7.3 572.1 %reduce-scatter.2.cloned.1.call-start = ((), (), s32[]{:S(2)}) async-start(), calls=%async_computation.1 | async-start | bytes 26214400 | tf_op jit(solution)/shard_map/reduce_scatter | solution.py:20
Sparse Core Ops, SparseCore 0:
  8.9 186.6 all-gather.2
  233.8 345.5 reduce-scatter.1
where the time goes:
time: 648 us
  waiting for transfers between devices  535 us (83%)
  matrix products  48 us (7%)
  blocking collectives  41.7 us (6%)
  between operations  14.1 us (2%)
    reduce_scatter x1, waiting for transfers between devices, body(): lax.psum_scatter(lax.dot_general(block, first, (((0,), (1,)), ((), ())),...  346 us
    all_gather x1, waiting for transfers between devices, body(): lax.all_gather(gradient, 'shard', axis=1, tiled=True)  188 us
    psum x1, blocking collectives, body(): total = lax.psum(squares, ('grp', 'shard'))  41.7 us
    dot_general x1, matrix products, body(): lax.dot_general(block, first, (((0,), (1,)), ((), ())), preferred_element...  20.6 us
    dot_general x1, matrix products, body(): lax.dot_general(lax.all_gather(gradient, 'shard', axis=1, tiled=True), bl...  17.5 us
  transfers between devices with their start and end apart: 2, of which 2 were waited for; matrix products, arithmetic and copies ran while one was open for 0% of the time, Pallas kernels for 0%

commit v1 on v0

v1 whole, which is shorter than its diff:
```python
import functools

import jax
import jax.numpy as jnp
from jax import lax
from jax.experimental import pallas as pl
from jax.experimental.pallas import tpu as pltpu
from jax.sharding import PartitionSpec as P

MESH = pl.DeviceIdType.MESH
VMEM_BYTES = 67_000_000
AHEAD = 2


def plain_body(gradients, left_factor, right_factor):
    gradient = gradients[0]
    left_q = left_factor[0]
    block = right_factor[0]
    first = lax.dot_general(
        lax.all_gather(gradient, "shard", axis=1, tiled=True),
        block,
        (((1,), (1,)), ((), ())),
        preferred_element_type=jnp.float32,
    ).astype(jnp.bfloat16)
    second_rows = lax.psum_scatter(
        lax.dot_general(block, first, (((0,), (1,)), ((), ())), preferred_element_type=jnp.float32),
        "shard",
        scatter_dimension=0,
        tiled=True,
    ).astype(jnp.bfloat16)
    second = second_rows.T
    third = jnp.dot(left_q, second, preferred_element_type=jnp.float32).astype(jnp.bfloat16)
    precond = lax.dot_general(
        left_q, third, (((0,), (0,)), ((), ())), preferred_element_type=jnp.float32
    )
    total = lax.psum(jnp.sum(precond * precond), ("grp", "shard"))
    count = precond.size * lax.axis_size("grp") * lax.axis_size("shard")
    rms = jnp.sqrt(total / count + 1e-06)
    factor = jnp.minimum(jnp.float32(1.0), 1.1 / rms)
    return (precond * factor).astype(jnp.bfloat16)[None]


def kernel(
    n, groups, m, g_hbm, q_hbm, r_hbm, out_hbm, factor_ref,
    gbuf, rbuf, qbuf, psend, precv, second, precond, acc, fst, thr, sq, sq_recv,
    load_sem, gsend, grecv, psend_sem, precv_sem, sq_send_sem, sq_recv_sem, out_sem,
):
    s = lax.axis_index("shard")
    g = lax.axis_index("grp")
    height, width = g_hbm.shape
    chunks = height // m
    lower = lax.rem(s + n - 1, n)
    upper = lax.rem(s + 1, n)

    def rows(t):
        return pl.ds(pl.multiple_of((chunks - 1 - t) * m, m), m)

    def load_r(d):
        cols = pl.ds(pl.multiple_of((s + d) * width, 128), width)
        return pltpu.make_async_copy(r_hbm.at[:, cols], rbuf.at[d], load_sem.at[d])

    load_g = pltpu.make_async_copy(g_hbm, gbuf.at[0], load_sem.at[n])
    load_q = pltpu.make_async_copy(q_hbm, qbuf, load_sem.at[n + 1])
    load_g.start()
    for d in range(n):
        pl.when(s + d < n)(lambda d=d: load_r(d).start())
    load_q.start()

    barrier = pltpu.get_barrier_semaphore()
    for o in range(1, n):
        pl.semaphore_signal(barrier, inc=1, device_id={"shard": lax.rem(s + o, n)}, device_id_type=MESH)
    for o in range(1, groups):
        pl.semaphore_signal(barrier, inc=1, device_id={"grp": lax.rem(g + o, groups)}, device_id_type=MESH)
    pl.semaphore_wait(barrier, n - 1 + groups - 1)

    def g_copy(t, k):
        src = g_hbm.at[rows(t)] if k == 1 else gbuf.at[k - 1, rows(t)]
        return pltpu.make_async_remote_copy(
            src_ref=src, dst_ref=gbuf.at[k, rows(t)],
            send_sem=gsend.at[t, k - 1], recv_sem=grecv.at[t, k - 1],
            device_id={"shard": lower}, device_id_type=MESH,
        )

    def p_copy(t, d):
        return pltpu.make_async_remote_copy(
            src_ref=psend.at[d - 1, rows(t)], dst_ref=precv.at[d - 1, rows(t)],
            send_sem=psend_sem.at[t, d - 1], recv_sem=precv_sem.at[t, d - 1],
            device_id={"shard": upper}, device_id_type=MESH,
        )

    def forward(t):
        @pl.when(s >= 1)
        def _():
            g_copy(t, 1).start()
            for k in range(2, n):
                @pl.when(s + k - 1 < n)
                def _(k=k):
                    g_copy(t, k - 1).wait_recv()
                    g_copy(t, k).start()

    forward(0)
    second[...] = jnp.zeros_like(second)
    precond[...] = jnp.zeros_like(precond)
    for t in range(1, min(AHEAD, chunks)):
        forward(t)
    load_g.wait()
    for d in range(n):
        pl.when(s + d < n)(lambda d=d: load_r(d).wait())
    load_q.wait()

    def step(t, carry):
        pl.when(t + AHEAD < chunks)(lambda: forward(t + AHEAD))
        here = rows(t)
        acc[...] = jnp.zeros_like(acc)

        def first_part(d, carry):
            for k in range(1, n):
                pl.when((s == 0) & (d == k))(lambda k=k: g_copy(t, k).wait_recv())
            acc[...] += lax.dot_general(
                gbuf[d, here, :], rbuf[d], (((1,), (1,)), ((), ())),
                preferred_element_type=jnp.float32,
            )
            return carry

        lax.fori_loop(0, n - s, first_part, 0)
        fst[...] = acc[...].astype(fst.dtype)

        def second_part(i, carry):
            d = n - 1 - s - i
            acc[...] = jnp.dot(fst[...], rbuf[d], preferred_element_type=jnp.float32)

            @pl.when(s >= 1)
            def _():
                p_copy(t, d + 1).wait_recv()
                acc[...] += precv[d, here, :].astype(jnp.float32)

            @pl.when(d >= 1)
            def _():
                psend[d - 1, here, :] = acc[...].astype(psend.dtype)
                p_copy(t, d).start()

            @pl.when(d == 0)
            def _():
                second[here, :] = acc[...].astype(second.dtype)

            return carry

        lax.fori_loop(0, n - s, second_part, 0)

        tile = 256 if width % 256 == 0 else 128

        def left_part(i, carry):
            cols = pl.ds(pl.multiple_of(i * tile, tile), tile)
            third = jnp.dot(
                qbuf[here, :], second[:, cols], preferred_element_type=jnp.float32
            ).astype(jnp.bfloat16)
            precond[:, cols] += lax.dot_general(
                qbuf[here, :], third, (((0,), (0,)), ((), ())),
                preferred_element_type=jnp.float32,
            )
            return carry

        lax.fori_loop(0, width // tile, left_part, 0)
        return carry

    lax.fori_loop(0, chunks, step, 0)

    write = pltpu.make_async_copy(precond, out_hbm, out_sem)
    write.start()

    thr[...] = jnp.zeros_like(thr)

    def square(i, carry):
        part = precond[pl.ds(pl.multiple_of(i * m, m), m), :]
        thr[...] += jnp.sum((part * part).reshape(m // 8, 8, width), axis=0)
        return carry

    lax.fori_loop(0, chunks, square, 0)
    mine = thr[:, :128]
    for c in range(1, width // 128):
        mine += thr[:, c * 128:(c + 1) * 128]

    def exchange(stage, value, axis, index, size, base):
        sq[stage] = value
        copies = [
            pltpu.make_async_remote_copy(
                src_ref=sq.at[stage], dst_ref=sq_recv.at[base + o - 1],
                send_sem=sq_send_sem.at[base + o - 1], recv_sem=sq_recv_sem.at[base + o - 1],
                device_id={axis: lax.rem(index + o, size)}, device_id_type=MESH,
            )
            for o in range(1, size)
        ]
        for copy in copies:
            copy.start()
        for copy in copies:
            copy.wait()
        for o in range(1, size):
            value += sq_recv[base + o - 1]
        return value

    value = exchange(0, mine, "shard", s, n, 0)
    value = exchange(1, value, "grp", g, groups, n - 1)
    total = jnp.sum(value)
    count = height * width * n * groups
    rms = jnp.sqrt(jnp.full((8, 128), total) / count + 1e-06)
    factor_ref[...] = jnp.minimum(jnp.float32(1.0), 1.1 / rms)

    def drain(t, carry):
        for k in range(1, n):
            pl.when((s >= 1) & (s + k - 1 < n))(lambda k=k: g_copy(t, k).wait_send())
            pl.when(s + k < n)(lambda k=k: p_copy(t, k).wait_send())
        return carry

    lax.fori_loop(0, chunks, drain, 0)
    write.wait()


def fused_body(n, groups, m, gradients, left_factor, right_factor):
    height, width = gradients.shape[1:]
    chunks = height // m
    bf16, f32 = jnp.bfloat16, jnp.float32
    dma = pltpu.SemaphoreType.DMA
    peers = n - 1 + groups - 1
    precond, factor = pl.pallas_call(
        functools.partial(kernel, n, groups, m),
        out_shape=(
            jax.ShapeDtypeStruct((height, width), f32),
            jax.ShapeDtypeStruct((8, 128), f32),
        ),
        in_specs=[pl.BlockSpec(memory_space=pl.ANY)] * 3,
        out_specs=(
            pl.BlockSpec(memory_space=pl.ANY),
            pl.BlockSpec(memory_space=pltpu.VMEM),
        ),
        scratch_shapes=[
            pltpu.VMEM((n, height, width), bf16),
            pltpu.VMEM((n, width, width), bf16),
            pltpu.VMEM((height, height), bf16),
            pltpu.VMEM((n - 1, height, width), bf16),
            pltpu.VMEM((n - 1, height, width), bf16),
            pltpu.VMEM((height, width), bf16),
            pltpu.VMEM((height, width), f32),
            pltpu.VMEM((m, width), f32),
            pltpu.VMEM((m, width), bf16),
            pltpu.VMEM((8, width), f32),
            pltpu.VMEM((2, 8, 128), f32),
            pltpu.VMEM((peers, 8, 128), f32),
            dma((n + 2,)),
            dma((chunks, n - 1)),
            dma((chunks, n - 1)),
            dma((chunks, n - 1)),
            dma((chunks, n - 1)),
            dma((peers,)),
            dma((peers,)),
            dma,
        ],
        compiler_params=pltpu.CompilerParams(
            collective_id=0, has_side_effects=True, vmem_limit_bytes=VMEM_BYTES
        ),
        name="kron_precondition",
    )(gradients[0], left_factor[0], right_factor[0])
    return (precond * factor[0, 0]).astype(jnp.bfloat16)[None]


def solution(mesh):
    n, groups = mesh.shape["shard"], mesh.shape["grp"]
    m = 128

    def body(gradients, left_factor, right_factor):
        height, width = gradients.shape[1:]
        need = 2 * (n * width * width + height * height + (3 * n + 1) * height * width)
        fits = need < VMEM_BYTES - 8_000_000
        if gradients.shape[0] == 1 and n > 1 and groups > 1 and width % 128 == 0 and height % m == 0 and fits:
            return fused_body(n, groups, m, gradients, left_factor, right_factor)
        return plain_body(gradients, left_factor, right_factor)

    in_specs = (P("grp", None, "shard"), P("grp", None, None), P("grp", "shard", None))
    out_specs = P("grp", None, "shard")
    return jax.shard_map(body, mesh=mesh, in_specs=in_specs, out_specs=out_specs, check_vma=False)
```

time: 648 us -> 279 us (0.43)
  waiting for transfers between devices: 535 us -> 0 us
  Pallas kernels: 0 us -> 273 us
  matrix products: 48 us -> 0 us
  blocking collectives: 41.7 us -> 0 us
  between operations: 14.1 us -> 0.01 us
    reduce_scatter x1 -> x0, waiting for transfers between devices: 346 us -> none  [body(): lax.psum_scatter(lax.dot_general(block, first, (((0,), (1,)), ((), ())),...]
    pallas_call x0 -> x1, Pallas kernels: none -> 273 us  [fused_body(): pl.pallas_call(functools.partial(kernel, n, groups, m), out_shape=(jax.Sh...]
    all_gather x1 -> x0, waiting for transfers between devices: 188 us -> none  [body(): lax.all_gather(gradient, 'shard', axis=1, tiled=True)]
    dot_general x3 -> x0, matrix products: 48 us -> none  [the longest x1 20.6 us: body(): lax.dot_general(block, first, (((0,), (1,)), ((), ())), preferred_element...]
    psum x1 -> x0, blocking collectives: 41.7 us -> none  [body(): total = lax.psum(squares, ('grp', 'shard'))]
  transfers between devices with their start and end apart: 2 -> 0, of which waited for: 2 -> 0; matrix products, arithmetic and copies ran while one was open for 0% -> 0% of each run, Pallas kernels for 0% -> 0%
where the time goes in v1:
time: 279 us
  Pallas kernels  273 us (98%)
  other arithmetic  5.06 us (2%)
    pallas_call x1, Pallas kernels, fused_body(): pl.pallas_call(functools.partial(kernel, n, groups, m), out_shape=(jax.Sh...  273 us

profile of v1, /device:TPU:0, one launch (start us, length us, event | category | flops | bytes accessed | tf_op | source)
XLA Modules:
  0.0 279.0 jit_solution(12454348095267027328)
XLA Ops:
  0.0 272.7 %kron_precondition.1 = (f32[1024,1280]{1,0:T(8,128)}, f32[8,128]{1,0:T(8,128)}) custom-call(bf16[1024,1280]{1,0:T(8,128)(2,1)} %bitcast.7, bf16[1024,1024]{1,0:T(8,128)(2,1)} %bitcast.8, bf16[1280,5120]{1,0:T(8,128)(2,1)} %bitcast.6), custom_call_target="tpu_custom_call" | custom-call | tf_op jit(solution)/shard_map/kron_precondition/pallas_call | solution.py:224
  272.7 1.3 slice.3
  273.9 5.1 %fusion = bf16[1,1024,1280]{2,1,0:T(8,128)(2,1)} fusion(f32[1024,1280]{1,0:T(8,128)} %get-tuple-element.7, f32[]{:T(128)} %bitcast.3), kind=kLoop, calls=%fused_computation.1 | loop fusion | flops 2621440 | bytes 7864324 | tf_op jit(solution)/shard_map/broadcast_in_dim | solution.py:262

commit v2 on v1

--- a/solution.py
+++ b/solution.py
@@ -9,7 +9,8 @@
 
 MESH = pl.DeviceIdType.MESH
 VMEM_BYTES = 67_000_000
-AHEAD = 2
+CHUNK_ROWS = 64
+AHEAD_PER_SHARD = 3
 
 
 def plain_body(gradients, left_factor, right_factor):
@@ -98,18 +99,23 @@
                     g_copy(t, k - 1).wait_recv()
                     g_copy(t, k).start()
 
-    forward(0)
+    ahead = jnp.where(s == n - 1, chunks, jnp.minimum(AHEAD_PER_SHARD * s, chunks))
+    pl.when(ahead >= 1)(lambda: forward(0))
     second[...] = jnp.zeros_like(second)
     precond[...] = jnp.zeros_like(precond)
-    for t in range(1, min(AHEAD, chunks)):
+
+    def early(t, carry):
         forward(t)
+        return carry
+
+    lax.fori_loop(1, ahead, early, 0)
     load_g.wait()
     for d in range(n):
         pl.when(s + d < n)(lambda d=d: load_r(d).wait())
     load_q.wait()
 
     def step(t, carry):
-        pl.when(t + AHEAD < chunks)(lambda: forward(t + AHEAD))
+        pl.when(t + ahead < chunks)(lambda: forward(t + ahead))
         here = rows(t)
         acc[...] = jnp.zeros_like(acc)
 
@@ -147,7 +153,7 @@
 
         lax.fori_loop(0, n - s, second_part, 0)
 
-        tile = 256 if width % 256 == 0 else 128
+        tile = width // 2 if width % 256 == 0 else 128
 
         def left_part(i, carry):
             cols = pl.ds(pl.multiple_of(i * tile, tile), tile)
@@ -264,7 +270,7 @@
 
 def solution(mesh):
     n, groups = mesh.shape["shard"], mesh.shape["grp"]
-    m = 128
+    m = CHUNK_ROWS
 
     def body(gradients, left_factor, right_factor):
         height, width = gradients.shape[1:]

time: 279 us -> 215 us (0.77)
  Pallas kernels: 273 us -> 209 us
    pallas_call x1, Pallas kernels: 273 us -> 209 us  [fused_body(): pl.pallas_call(functools.partial(kernel, n, groups, m), out_shape=(jax.Sh...]
where the time goes in v2:
time: 215 us
  Pallas kernels  209 us (97%)
  other arithmetic  5.06 us (2%)
    pallas_call x1, Pallas kernels, fused_body(): pl.pallas_call(functools.partial(kernel, n, groups, m), out_shape=(jax.Sh...  209 us
    broadcast_in_dim x1, other arithmetic, fused_body(): return (precond * factor[0, 0]).astype(jnp.bfloat16)[None]  5.06 us

profile of v2, /device:TPU:0, one launch (start us, length us, event | category | flops | bytes accessed | tf_op | source)
XLA Modules:
  0.0 214.9 jit_solution(12495813318049879343)
XLA Ops:
  0.0 208.5 %kron_precondition.1 = (f32[1024,1280]{1,0:T(8,128)}, f32[8,128]{1,0:T(8,128)}) custom-call(bf16[1024,1280]{1,0:T(8,128)(2,1)} %bitcast.7, bf16[1024,1024]{1,0:T(8,128)(2,1)} %bitcast.8, bf16[1280,5120]{1,0:T(8,128)(2,1)} %bitcast.6), custom_call_target="tpu_custom_call" | custom-call | tf_op jit(solution)/shard_map/kron_precondition/pallas_call | solution.py:230
  208.5 1.3 slice.3
  209.8 5.1 %fusion = bf16[1,1024,1280]{2,1,0:T(8,128)(2,1)} fusion(f32[1024,1280]{1,0:T(8,128)} %get-tuple-element.7, f32[]{:T(128)} %bitcast.3), kind=kLoop, calls=%fused_computation.1 | loop fusion | flops 2621440 | bytes 7864324 | tf_op jit(solution)/shard_map/broadcast_in_dim | solution.py:268
